TPU v7x, 32 devices: a whole 2x2x4 slice. The times are simulated.
32 devices in a mesh: seq: 8 (over z, y), head: 4 (over x, core).
Axes of the slice: x: 2, y: 2, z: 4, core: 2. Of those that a mesh axis runs over, the one named last changes fastest.
Arguments:
- query: bfloat16 [128, 32, 128], P(None, 'head'), may hold values from -8 to 8
- key_cache: bfloat16 [16384, 16, 128], P('seq', 'head'), may hold values from -6 to 6
- value_cache: bfloat16 [16384, 16, 128], P('seq', 'head'), may hold values from -6 to 6
- lengths: int32 [8], P('seq'), may hold values from 1 to 2048, 12288 in all
- out_weight: bfloat16 [4608, 4096], P('seq', 'head'), may hold values from -10 to 10
- norm_gain: float32 [4608], P('seq'), may hold values from 0.1 to 1.9
Outputs:
- normed: bfloat16 [128, 4608], P(None, 'seq')
Inputs may be any that keep to these rules, and one draw needn't show every extreme that they name: `lengths`: every block has at least one valid position, and some block is valid throughout.
All inputs are finite; a program needn't handle non-finite values.
Results may differ from a plain program's by a relative error of at most 0.0083.
Values may be sent and summed in bfloat16 or wider, within the bound.
A program may use at most 128 MiB of HBM per device.

v0:
```python
import jax
import jax.numpy as jnp
from jax import lax
from jax.sharding import PartitionSpec as P

D = 4608
QPRE = 144


def merged(value, axis, join):
    pieces = jax.tree.map(lambda part: lax.all_gather(part, axis), value)
    head = jax.tree.map(lambda part: part[0], pieces)
    tail = jax.tree.map(lambda part: part[1:], pieces)
    so_far, _ = lax.scan(lambda so_far, share: (join(so_far, share), None), head, tail)
    return so_far


def combine_partials(former, latter):
    max_former, sum_former, acc_former = former
    max_latter, sum_latter, acc_latter = latter
    new_max = jnp.maximum(max_former, max_latter)
    factor_former = jnp.exp(max_former - new_max)
    factor_latter = jnp.exp(max_latter - new_max)
    new_sum = factor_former * sum_former + factor_latter * sum_latter
    new_acc = factor_former[..., None] * acc_former + factor_latter[..., None] * acc_latter
    return (new_max, new_sum, new_acc)


def body(query, key_cache, value_cache, lengths, out_weight, norm_gain):
    tok_count, heads_local, head_dim = query.shape
    key_count, kv_local, unused_dim = key_cache.shape
    group_size = heads_local // kv_local
    score_scale = float(QPRE) ** (-0.5)
    grouped = query.reshape(tok_count, kv_local, group_size, head_dim)
    scores = (
        jnp.einsum("tkgd,ckd->kgtc", grouped, key_cache, preferred_element_type=jnp.float32)
        * score_scale
    )
    inside = lax.iota(jnp.int32, key_count) < lengths[0]
    scores = jnp.where(inside, scores, jnp.float32(-1e30))
    block_max = jnp.max(scores, axis=-1)
    weights = jnp.where(inside, jnp.exp(scores - block_max[..., None]), jnp.float32(0.0))
    block_sum = jnp.sum(weights, axis=-1)
    weights_low = weights.astype(jnp.bfloat16)
    weighted = jnp.einsum(
        "kgtc,ckd->tkgd", weights_low, value_cache, preferred_element_type=jnp.float32
    )
    weighted = weighted.reshape(tok_count, heads_local, head_dim)
    block_max = jnp.transpose(block_max, (2, 0, 1)).reshape(tok_count, heads_local)
    block_sum = jnp.transpose(block_sum, (2, 0, 1)).reshape(tok_count, heads_local)
    peak_all, total_all, combined = merged(
        (block_max, block_sum, weighted), "seq", combine_partials
    )
    attention = (
        (combined / total_all[..., None])
        .reshape(tok_count, heads_local * head_dim)
        .astype(jnp.bfloat16)
    )
    projected_part = lax.dot_general(
        attention, out_weight, (((1,), (1,)), ((), ())), preferred_element_type=jnp.float32
    )
    projected = lax.psum(projected_part, "head")
    square_part = jnp.sum(projected * projected, axis=-1)
    square_total = lax.psum(square_part, "seq")
    mean_square = square_total / D
    normed = projected * lax.rsqrt(mean_square + 1e-06)[:, None] * norm_gain[None, :]
    return normed.astype(jnp.bfloat16)


def solution(mesh):
    placed = (
        P(None, "head", None),
        P("seq", "head", None),
        P("seq", "head", None),
        P("seq"),
        P("seq", "head"),
        P("seq"),
    )
    return jax.shard_map(
        body, mesh=mesh, in_specs=placed, out_specs=P(None, "seq"), check_vma=False
    )
```

profile of v0, /device:TPU:0, one launch (start us, length us, event | category | flops | bytes accessed | tf_op | source)
XLA Modules:
  0.0 174.1 jit_solution(1487944032741304655)
XLA Ops:
  7.4 3.9 %bitcast_reduce_fusion = (f32[4,2,128]{2,1,0:T(2,128)S(1)}, f32[4,2048,128,2]{2,1,3,0:T(8,128)S(1)}) fusion(pred[2048]{0:T(1024)(128)(4,1)S(1)} %iota_compare_fusion, bf16[128,4,2,128]{3,2,1,0:T(2,128)(2,1)} %bitcast.62, bf16[2048,4,128,1]{2,1,0,3:T(4,128)(2,1)} %bitcast.61), kind=kOutput, calls=%fused_computation.9 | convolution fusion | flops 543161344 | bytes 10754048 | tf_op jit(solution)/shard_map/tkgd,ckd->kgtc/dot_general | solution.py:36
  11.2 3.4 %fusion.7 = f32[4,2,128,128]{3,2,1,0:T(8,128)S(1)} fusion(f32[4,2048,128,2]{2,1,3,0:T(8,128)S(1)} %get-tuple-element.64, f32[4,2,128]{2,1,0:T(2,128)S(1)} %get-tuple-element.63, pred[2048]{0:T(1024)(128)(4,1)S(1)} %iota_compare_fusion, bf16[2048,4,128,1]{2,1,0,3:T(4,128)(2,1)S(1)} %bitcast.56), kind=kOutput, calls=%fused_computation.15 | convolution fusion | flops 547356672 | bytes 11016192 | tf_op jit(solution)/shard_map/kgtc,ckd->tkgd/dot_general | solution.py:45
  14.7 1.1 copy.21
  15.9 4.6 %fusion.6 = f32[4,2,128]{2,1,0:T(2,128)S(1)} fusion(f32[4,2048,128,2]{2,1,3,0:T(8,128)} %copy-done.1, f32[4,2,128]{2,1,0:T(2,128)S(1)} %get-tuple-element.63, pred[2048]{0:T(1024)(128)(4,1)S(1)} %iota_compare_fusion), kind=kLoop, calls=%fused_computation.14 | loop fusion | flops 10484736 | bytes 8398848 | tf_op jit(solution)/shard_map/reduce_sum | solution.py:43
  20.5 33.0 %all_gather.10 = f32[8,128,8]{1,2,0:T(8,128)S(1)} all-gather(f32[1,128,8]{1,2,0:T(8,128)S(1)} %bitcast.60), channel_id=1, replica_groups=mesh['seq'=8,'head'=4] {'seq'}, dimensions={0}, use_global_device_ids=true | all-gather | bytes 36864 | tf_op jit(solution)/shard_map/all_gather | solution.py:11
  53.5 31.8 %all_gather.9 = f32[8,128,8]{1,2,0:T(8,128)S(1)} all-gather(f32[1,128,8]{1,2,0:T(8,128)S(1)} %bitcast.59), channel_id=1, replica_groups=mesh['seq'=8,'head'=4] {'seq'}, dimensions={0}, use_global_device_ids=true | all-gather | bytes 36864 | tf_op jit(solution)/shard_map/all_gather | solution.py:11
  85.3 6.9 %all-gather.2.cloned.1.call-done = f32[8,128,8,128]{3,2,1,0:T(8,128)} async-done(((f32[1,128,8,128]{3,2,1,0:T(8,128)}), f32[8,128,8,128]{3,2,1,0:T(8,128)}) %all-gather.2.cloned.1.call-update) | async-done | bytes 4194320 | tf_op jit(solution)/shard_map/all_gather | solution.py:11
  92.2 1.1 slice_bitcast_fusion
  93.3 4.1 %slice.29 = f32[7,128,8,128]{3,2,1,0:T(8,128)} slice(f32[8,128,8,128]{3,2,1,0:T(8,128)} %all-gather.2.cloned.1.call-done), slice={[1:8], [0:128], [0:8], [0:128]} | slice | bytes 7340032 | tf_op jit(solution)/shard_map/slice | solution.py:13
  97.4 11.7 %while.14 = (s32[]{:T(128)}, f32[128,8]{0,1:T(8,128)S(1)}, f32[128,8]{0,1:T(8,128)S(1)}, f32[128,8,128]{2,1,0:T(8,128)S(1)}, f32[7,128,8]{1,2,0:T(8,128)S(1)}, /...) while((s32[]{:T(128)}, f32[128,8]{0,1:T(8,128)S(1)}, f32[128,8]{0,1:T(8,128)S(1)}, ...), condition=%wide.region_3.4_spmd, body=%wide.region_2.3_spmd.sunk | while | flops 399362 | bytes 1630309 | solution.py:14
  97.4 0.1 copy.47
  97.6 1.4 fusion.26
  99.3 1.4 fusion.26
  100.9 1.4 fusion.26
  102.6 1.4 fusion.26
  104.3 1.4 fusion.26
  106.0 1.4 fusion.26
  107.7 1.4 fusion.26
  109.2 0.2 divide_convert_fusion
  109.4 2.5 %fusion.14 = f32[128,576]{0,1:T(8,128)} fusion(bf16[576,1024]{1,0:T(8,128)(2,1)} %param.12, bf16[16,8,8,128]{3,2,1,0:T(8,128)(2,1)S(1)} %bitcast.57), kind=kOutput, calls=%fused_computation.25 | convolution fusion | flops 150994944 | bytes 1736704 | tf_op jit(solution)/shard_map/dot_general | solution.py:59
  111.9 31.2 %all-reduce.2.cloned.1.call-done = f32[128,576]{0,1:T(8,128)} async-done(((f32[128,576]{0,1:T(8,128)}), f32[128,576]{0,1:T(8,128)}) %all-reduce.2.cloned.1.call-update) | async-done | bytes 294928 | tf_op jit(solution)/shard_map/psum | solution.py:62
  143.1 1.1 multiply_reduce_fusion
  144.2 21.4 %psum.15 = f32[128]{0:T(128)S(1)} all-reduce(f32[128]{0:T(128)S(1)} %multiply_reduce_fusion), channel_id=1, replica_groups=mesh['seq'=8,'head'=4] {'seq'}, use_global_device_ids=true, to_apply=%region_6.7 | all-reduce | flops 128 | bytes 1024 | tf_op jit(solution)/shard_map/psum | solution.py:64
  165.5 1.8 %multiply_convert_fusion = bf16[128,576]{0,1:T(8,128)(2,1)} fusion(f32[128,576]{0,1:T(8,128)} %all-reduce.2.cloned.1.call-done, f32[576]{0:T(1024)S(1)} %copy-done.2, f32[128]{0:T(128)S(1)} %add_rsqrt_fusion), kind=kLoop, calls=%fused_computation.23 | loop fusion | flops 221184 | bytes 445184 | tf_op jit(solution)/shard_map/convert_element_type | solution.py:67
  (37 shorter events, 1.7 us)
Async XLA Ops:
  6.5 4.7 %copy-start = (bf16[2048,4,128]{2,1,0:T(4,128)(2,1)S(1)}, bf16[2048,4,128]{2,1,0:T(4,128)(2,1)}, u32[]{:S(2)}) copy-start(bf16[2048,4,128]{2,1,0:T(4,128)(2,1)} %param.10) | copy-start | bytes 6291460
  6.5 85.7 %all-gather.2.cloned.1.call-start = ((), (), s32[]{:S(2)}) async-start(), calls=%async_computation | async-start | bytes 4718592 | tf_op jit(solution)/shard_map/all_gather | solution.py:11
  11.2 3.5 %copy-start.1 = (f32[4,2048,128,2]{2,1,3,0:T(8,128)}, f32[4,2048,128,2]{2,1,3,0:T(8,128)S(1)}, u32[]{:S(2)}) copy-start(f32[4,2048,128,2]{2,1,3,0:T(8,128)S(1)} %get-tuple-element.64) | copy-start | bytes 25165828
  15.9 127.2 %all-reduce.2.cloned.1.call-start = ((), (), s32[]{:S(2)}) async-start(), calls=%async_computation.1 | async-start | bytes 589824 | tf_op jit(solution)/shard_map/psum | solution.py:62
  93.3 72.2 %copy-start.2 = (f32[576]{0:T(1024)S(1)}, f32[576]{0:T(1024)}, u32[]{:S(2)}) copy-start(f32[576]{0:T(1024)} %param.13) | copy-start | bytes 6916
Sparse Core Ops, SparseCore 0:
  16.0 76.1 all-gather.1
  112.0 31.0 all-reduce.1
where the time goes:
time: 175 us; the launch traced here: 174 us
  blocking collectives  86.2 us (49%)
  waiting for transfers between devices  38.1 us (22%)
  other arithmetic  17.8 us (10%)
  between operations  14.3 us (8%)
  matrix products  9.75 us (6%)
  local copies, waits for them, and re-layouts  7.82 us (4%)
    all_gather x2, blocking collectives, merged(): pieces = jax.tree.map(lambda part: lax.all_gather(part, axis), value)  64.8 us
    psum x1, waiting for transfers between devices, body(): projected = lax.psum(projected_part, 'head')  31.2 us
    psum x1, blocking collectives, body(): square_total = lax.psum(square_part, 'seq')  21.4 us
    add x7, other arithmetic, combine_partials(): factor_former[..., None] * acc_former  10 us
    all_gather x1, waiting for transfers between devices, merged(): pieces = jax.tree.map(lambda part: lax.all_gather(part, axis), value)  6.87 us
    reduce_sum x1, other arithmetic, body(): block_sum = jnp.sum(weights, axis=-1)  4.59 us
    slice x3, local copies, waits for them, and re-layouts, merged(): tail = jax.tree.map(lambda part: part[1:], pieces)  4.08 us
    dot_general x1, matrix products, body(): jnp.einsum('tkgd,ckd->kgtc', grouped, key_cache, preferred_element_type=j...  3.86 us
  transfers between devices with their start and end apart: 2, of which 2 were waited for; matrix products, arithmetic and copies ran while one was open for 3% of the time, Pallas kernels for 0%

commit v1 on v0

--- a/solution.py
+++ b/solution.py
@@ -59,7 +59,7 @@
     projected_part = lax.dot_general(
         attention, out_weight, (((1,), (1,)), ((), ())), preferred_element_type=jnp.float32
     )
-    projected = lax.psum(projected_part, "head")
+    projected = jnp.sum(lax.all_gather(projected_part, "head"), axis=0)
     square_part = jnp.sum(projected * projected, axis=-1)
     square_total = lax.psum(square_part, "seq")
     mean_square = square_total / D

time: 175 us -> 163 us (0.931)
  waiting for transfers between devices: 38.1 us -> 23.2 us
    psum x1 -> x0, waiting for transfers between devices: 31.2 us -> none  [body(): projected = lax.psum(projected_part, 'head')]
    all_gather x0 -> x1, waiting for transfers between devices: none -> 16.3 us  [body(): projected = jnp.sum(lax.all_gather(projected_part, 'head'), axis=0)]
where the time goes in v1:
time: 163 us; the launch traced here: 162 us
  blocking collectives  86.2 us (53%)
  waiting for transfers between devices  23.2 us (14%)
  other arithmetic  19.2 us (12%)
  between operations  14.3 us (9%)
  matrix products  9.78 us (6%)
  local copies, waits for them, and re-layouts  9.47 us (6%)
    all_gather x2, blocking collectives, merged(): pieces = jax.tree.map(lambda part: lax.all_gather(part, axis), value)  64.8 us
    psum x1, blocking collectives, body(): square_total = lax.psum(square_part, 'seq')  21.4 us
    all_gather x1, waiting for transfers between devices, body(): projected = jnp.sum(lax.all_gather(projected_part, 'head'), axis=0)  16.3 us
    add x7, other arithmetic, combine_partials(): factor_former[..., None] * acc_former  10 us
    all_gather x1, waiting for transfers between devices, merged(): pieces = jax.tree.map(lambda part: lax.all_gather(part, axis), value)  6.87 us
    reduce_sum x1, other arithmetic, body(): block_sum = jnp.sum(weights, axis=-1)  4.59 us
    slice x3, local copies, waits for them, and re-layouts, merged(): tail = jax.tree.map(lambda part: part[1:], pieces)  4.08 us
    dot_general x1, matrix products, body(): jnp.einsum('tkgd,ckd->kgtc', grouped, key_cache, preferred_element_type=j...  3.86 us
  transfers between devices with their start and end apart: 2, of which 2 were waited for; matrix products, arithmetic and copies ran while one was open for 3% of the time, Pallas kernels for 0%

profile of v1, /device:TPU:0, one launch (start us, length us, event | category | flops | bytes accessed | tf_op | source)
XLA Modules:
  0.0 162.3 jit_solution(6585406153136113833)
XLA Ops:
  7.4 3.9 %bitcast_reduce_fusion = (f32[4,2,128]{2,1,0:T(2,128)S(1)}, f32[4,2048,128,2]{2,1,3,0:T(8,128)S(1)}) fusion(pred[2048]{0:T(1024)(128)(4,1)S(1)} %iota_compare_fusion, bf16[128,4,2,128]{3,2,1,0:T(2,128)(2,1)} %bitcast.64, bf16[2048,4,128,1]{2,1,0,3:T(4,128)(2,1)} %bitcast.63), kind=kOutput, calls=%fused_computation.9 | convolution fusion | flops 543161344 | bytes 10754048 | tf_op jit(solution)/shard_map/tkgd,ckd->kgtc/dot_general | solution.py:36
  11.2 3.4 %fusion.7 = f32[4,2,128,128]{3,2,1,0:T(8,128)S(1)} fusion(f32[4,2048,128,2]{2,1,3,0:T(8,128)S(1)} %get-tuple-element.64, f32[4,2,128]{2,1,0:T(2,128)S(1)} %get-tuple-element.63, pred[2048]{0:T(1024)(128)(4,1)S(1)} %iota_compare_fusion, bf16[2048,4,128,1]{2,1,0,3:T(4,128)(2,1)S(1)} %bitcast.58), kind=kOutput, calls=%fused_computation.15 | convolution fusion | flops 547356672 | bytes 11016192 | tf_op jit(solution)/shard_map/kgtc,ckd->tkgd/dot_general | solution.py:45
  14.7 1.1 copy.21
  15.9 4.6 %fusion.6 = f32[4,2,128]{2,1,0:T(2,128)S(1)} fusion(f32[4,2048,128,2]{2,1,3,0:T(8,128)} %copy-done.1, f32[4,2,128]{2,1,0:T(2,128)S(1)} %get-tuple-element.63, pred[2048]{0:T(1024)(128)(4,1)S(1)} %iota_compare_fusion), kind=kLoop, calls=%fused_computation.14 | loop fusion | flops 10484736 | bytes 8398848 | tf_op jit(solution)/shard_map/reduce_sum | solution.py:43
  20.5 33.0 %all_gather.16 = f32[8,128,8]{1,2,0:T(8,128)S(1)} all-gather(f32[1,128,8]{1,2,0:T(8,128)S(1)} %bitcast.62), channel_id=1, replica_groups=mesh['seq'=8,'head'=4] {'seq'}, dimensions={0}, use_global_device_ids=true | all-gather | bytes 36864 | tf_op jit(solution)/shard_map/all_gather | solution.py:11
  53.5 31.8 %all_gather.15 = f32[8,128,8]{1,2,0:T(8,128)S(1)} all-gather(f32[1,128,8]{1,2,0:T(8,128)S(1)} %bitcast.61), channel_id=1, replica_groups=mesh['seq'=8,'head'=4] {'seq'}, dimensions={0}, use_global_device_ids=true | all-gather | bytes 36864 | tf_op jit(solution)/shard_map/all_gather | solution.py:11
  85.3 6.9 %all-gather.4.cloned.1.call-done = f32[8,128,8,128]{3,2,1,0:T(8,128)} async-done(((f32[1,128,8,128]{3,2,1,0:T(8,128)}), f32[8,128,8,128]{3,2,1,0:T(8,128)}) %all-gather.4.cloned.1.call-update) | async-done | bytes 4194320 | tf_op jit(solution)/shard_map/all_gather | solution.py:11
  92.2 1.1 slice_bitcast_fusion
  93.3 4.1 %slice.29 = f32[7,128,8,128]{3,2,1,0:T(8,128)} slice(f32[8,128,8,128]{3,2,1,0:T(8,128)} %all-gather.4.cloned.1.call-done), slice={[1:8], [0:128], [0:8], [0:128]} | slice | bytes 7340032 | tf_op jit(solution)/shard_map/slice | solution.py:13
  97.4 11.7 %while.14 = (s32[]{:T(128)}, f32[128,8]{0,1:T(8,128)S(1)}, f32[128,8]{0,1:T(8,128)S(1)}, f32[128,8,128]{2,1,0:T(8,128)S(1)}, f32[7,128,8]{1,2,0:T(8,128)S(1)}, /...) while((s32[]{:T(128)}, f32[128,8]{0,1:T(8,128)S(1)}, f32[128,8]{0,1:T(8,128)S(1)}, ...), condition=%wide.region_3.4_spmd, body=%wide.region_2.3_spmd.sunk | while | flops 399362 | bytes 1630309 | solution.py:14
  97.6 1.4 fusion.26
  99.2 1.4 fusion.26
  100.9 1.4 fusion.26
  102.6 1.4 fusion.26
  104.3 1.4 fusion.26
  106.0 1.4 fusion.26
  107.6 1.4 fusion.26
  109.4 2.5 %fusion.14 = f32[128,576]{0,1:T(8,128)} fusion(bf16[576,1024]{1,0:T(8,128)(2,1)} %param.12, bf16[16,8,8,128]{3,2,1,0:T(8,128)(2,1)S(1)} %bitcast.59), kind=kOutput, calls=%fused_computation.25 | convolution fusion | flops 150994944 | bytes 1736704 | tf_op jit(solution)/shard_map/dot_general | solution.py:59
  111.9 16.3 %all-gather.6.cloned.1.call-done = f32[512,576]{0,1:T(8,128)} async-done(((f32[128,576]{0,1:T(8,128)}), f32[512,576]{0,1:T(8,128)}) %all-gather.6.cloned.1.call-update) | async-done | bytes 1179664 | tf_op jit(solution)/shard_map/all_gather | solution.py:62
  128.2 1.7 %reshape.12 = f32[4,128,576]{1,0,2:T(4,128)S(1)} reshape(f32[512,576]{0,1:T(8,128)} %all-gather.6.cloned.1.call-done) | data formatting | bytes 2359296 | tf_op jit(solution)/shard_map/all_gather | solution.py:62
  129.8 1.4 reduce_sum.28
  131.3 1.1 multiply_reduce_fusion
  132.3 21.4 %psum.7 = f32[128]{0:T(128)S(1)} all-reduce(f32[128]{0:T(128)S(1)} %multiply_reduce_fusion), channel_id=1, replica_groups=mesh['seq'=8,'head'=4] {'seq'}, use_global_device_ids=true, to_apply=%region_6.7 | all-reduce | flops 128 | bytes 1024 | tf_op jit(solution)/shard_map/psum | solution.py:64
  153.7 1.8 %multiply_convert_fusion = bf16[128,576]{0,1:T(8,128)(2,1)} fusion(f32[128,576]{0,1:T(8,128)} %reduce_sum.28, f32[576]{0:T(1024)S(1)} %copy-done.2, f32[128]{0:T(128)S(1)} %add_rsqrt_fusion), kind=kLoop, calls=%fused_computation.23 | loop fusion | flops 221184 | bytes 445184 | tf_op jit(solution)/shard_map/convert_element_type | solution.py:67
  (39 shorter events, 1.9 us)
Async XLA Ops:
  6.5 4.7 %copy-start = (bf16[2048,4,128]{2,1,0:T(4,128)(2,1)S(1)}, bf16[2048,4,128]{2,1,0:T(4,128)(2,1)}, u32[]{:S(2)}) copy-start(bf16[2048,4,128]{2,1,0:T(4,128)(2,1)} %param.10) | copy-start | bytes 6291460
  6.5 85.7 %all-gather.4.cloned.1.call-start = ((), (), s32[]{:S(2)}) async-start(), calls=%async_computation | async-start | bytes 4718592 | tf_op jit(solution)/shard_map/all_gather | solution.py:11
  11.2 3.5 %copy-start.1 = (f32[4,2048,128,2]{2,1,3,0:T(8,128)}, f32[4,2048,128,2]{2,1,3,0:T(8,128)S(1)}, u32[]{:S(2)}) copy-start(f32[4,2048,128,2]{2,1,3,0:T(8,128)S(1)} %get-tuple-element.64) | copy-start | bytes 25165828
  15.9 112.3 %all-gather.6.cloned.1.call-start = ((), (), s32[]{:S(2)}) async-start(), calls=%async_computation.1 | async-start | bytes 1474560 | tf_op jit(solution)/shard_map/all_gather | solution.py:62
  97.4 56.4 %copy-start.2 = (f32[576]{0:T(1024)S(1)}, f32[576]{0:T(1024)}, u32[]{:S(2)}) copy-start(f32[576]{0:T(1024)} %param.13) | copy-start | bytes 6916
Sparse Core Ops, SparseCore 0:
  16.0 76.1 all-gather.3
  112.0 16.1 all-gather.5
